TPU v7x, 32 devices: a whole 2x2x4 slice. The times are simulated.
32 devices in a mesh: row: 4 (over y, core), col: 8 (over z, x).
Axes of the slice: x: 2, y: 2, z: 4, core: 2. Of those that a mesh axis runs over, the one named last changes fastest.
Arguments:
- residuals: bfloat16 [16384, 32], P(('row', 'col')), may hold values from -6 to 6
- intersect_blocks: int32 [32, 4], P(('row', 'col')), may hold values from 0 to 3
- local_inverse: bfloat16 [16384, 1024], P(('row', 'col')), may hold values from -0.1875 to 0.1875
- coarse_basis: float32 [32768, 64], P(('row', 'col')), may hold values from -0.1875 to 0.1875
- coarse_slots: int32 [2048], replicated, may hold values from 0 to 2047, each once
- coarse_inverse: float32 [2048, 2048], P('row', 'col'), may hold values from -0.5 to 0.5
Outputs:
- preconditioned: float32 [16384, 32], P(('row', 'col'))
Inputs may be any that keep to these rules, and one draw needn't show every extreme that they name: `intersect_blocks`: each entry names one of the four owned blocks. `coarse_slots`: every coarse index from 0 to 2047 appears exactly once.
All inputs are finite; a program needn't handle non-finite values.
Results may differ from a plain program's by a relative error of at most 0.0003.
Values may be sent and summed in bfloat16 or wider, within the bound.
A program may use at most 64 MiB of HBM per device.

v0:
```python
import jax
import jax.numpy as jnp
from jax import lax
from jax.sharding import PartitionSpec as P

BLK = 128


def extended(cells, sides, width, closed):
    for axis, dim in sides:
        count = lax.axis_size(axis)
        ends = count if closed else count - 1
        head = lax.slice_in_dim(cells, 0, width, axis=dim)
        tail = lax.slice_in_dim(cells, cells.shape[dim] - width, cells.shape[dim], axis=dim)
        cells = jnp.concatenate(
            [
                lax.ppermute(tail, axis, [(i, (i + 1) % count) for i in range(ends)]),
                cells,
                lax.ppermute(head, axis, [((i + 1) % count, i) for i in range(ends)]),
            ],
            axis=dim,
        )
    return cells


def shards(residuals, intersect_blocks, local_inverse, coarse_basis, coarse_slots, coarse_inverse):
    own_rows = residuals.shape[0]
    rhs_count = residuals.shape[1]
    nev_count = coarse_basis.shape[1]
    blocks = residuals.reshape(own_rows // BLK, BLK, rhs_count)
    send_index = intersect_blocks[0]
    outgoing = jnp.take(blocks, send_index, axis=0)
    padded = extended(outgoing[None, None], (("row", 0), ("col", 1)), 1, False)
    incoming = jnp.stack([padded[0, 1, 0], padded[2, 1, 1], padded[1, 0, 2], padded[1, 2, 3]])
    local_vec = jnp.concatenate([residuals, incoming.reshape(-1, rhs_count)], axis=0)
    schwarz = jnp.dot(local_inverse, local_vec, preferred_element_type=jnp.float32)
    partial_sums = jnp.dot(
        coarse_basis.T, local_vec.astype(jnp.float32), precision=lax.Precision.HIGHEST
    )
    column_width = coarse_inverse.shape[1]
    col_offset = lax.axis_index("col") * column_width

    def add_piece(carry, piece):
        shifted = lax.slice_in_dim(coarse_slots, 0, piece.shape[0], axis=0) - col_offset
        inside = (shifted >= 0) & (shifted < column_width)
        target = jnp.where(inside, shifted, column_width)
        return carry.at[target].add(piece, mode="drop")

    column_part = add_piece(
        jnp.zeros((column_width, rhs_count), jnp.float32),
        jax.tree.map(lambda a: lax.all_gather(a, ("row", "col"), axis=0, tiled=True), partial_sums),
    )
    product = jnp.dot(coarse_inverse, column_part, precision=lax.Precision.HIGHEST)
    row_total = lax.psum(product, "col")
    whole_coarse = lax.all_gather(row_total, "row", axis=0, tiled=True)
    my_slots = lax.dynamic_slice_in_dim(
        coarse_slots, lax.axis_index(("row", "col")) * nev_count, nev_count, 0
    )
    own_coarse = jnp.take(whole_coarse, my_slots, axis=0)
    prolonged = jnp.dot(coarse_basis, own_coarse, precision=lax.Precision.HIGHEST)
    returning = prolonged[own_rows:].reshape(-1, BLK, rhs_count)
    padded_back = extended(returning[None, None], (("row", 0), ("col", 1)), 1, False)
    returned = jnp.stack(
        [padded_back[2, 1, 0], padded_back[0, 1, 1], padded_back[1, 2, 2], padded_back[1, 0, 3]]
    )
    matches = (send_index[:, None] == jnp.arange(own_rows // BLK, dtype=jnp.int32)[None, :]).astype(
        jnp.float32
    )
    added = jnp.einsum("db,dkr->bkr", matches, returned, precision=lax.Precision.HIGHEST)
    return schwarz + prolonged[:own_rows] + added.reshape(own_rows, rhs_count)


def solution(mesh):
    placed = (
        P(("row", "col"), None),
        P(("row", "col"), None),
        P(("row", "col"), None),
        P(("row", "col"), None),
        P(),
        P("row", "col"),
    )
    return jax.shard_map(
        shards, mesh=mesh, in_specs=placed, out_specs=P(("row", "col"), None), check_vma=False
    )
```

profile of v0, /device:TPU:0, one launch (start us, length us, event | category | flops | bytes accessed | tf_op | source)
XLA Modules:
  0.0 212.6 jit_solution(17657866889500280651)
XLA Ops:
  6.5 0.8 fusion.18
  7.3 0.8 copy_bitcast_fusion
  8.1 0.6 gather_fusion
  8.8 2.4 %collective-permute-start = (bf16[1,1,4,128,32]{3,4,2,1,0:T(8,128)(2,1)S(1)}, bf16[1,1,4,128,32]{3,4,2,1,0:T(8,128)(2,1)S(1)}, u32[]{:S(2)}, u32[]{:S(2)}) collective-permute-start(bf16[1,1,4,128,32]{3,4,2,1,0:T(8,128)(2,1)S(1)} %bitcast_select_fusion), channel_id=1, source_target_pairs={{0,8},{8,16},{16,24},{1,9},{9,17},{17,25},{2,10},{10,18},{18,26},{... | collective-permute-start | bytes 98312 | tf_op jit(solution)/shard_map/ppermute | solution.py:17
  11.2 1.3 collective-permute-start.1
  12.6 3.8 %collective-permute-done.1 = bf16[1,1,4,128,32]{3,4,2,1,0:T(8,128)(2,1)S(1)} collective-permute-done((bf16[1,1,4,128,32]{3,4,2,1,0:T(8,128)(2,1)S(1)}, bf16[1,1,4,128,32]{3,4,2,1,0:T(8,128)(2,1)S(1)}, u32[]{:S(2)}, u32[]{:S(2)}) %collective-permute-start.1) | collective-permute-done | bytes 32800 | tf_op jit(solution)/shard_map/ppermute | solution.py:19
  16.4 1.3 collective-permute-start.3
  17.7 4.6 %collective-permute-start.2 = (bf16[3,1,4,128,32]{3,4,2,1,0:T(8,128)(2,1)S(1)}, bf16[3,1,4,128,32]{3,4,2,1,0:T(8,128)(2,1)S(1)}, u32[]{:S(2)}, u32[]{:S(2)}) collective-permute-start(bf16[3,1,4,128,32]{3,4,2,1,0:T(8,128)(2,1)S(1)} %pad_maximum_fusion), channel_id=1, source_target_pairs={{0,1},{1,2},{2,3},{3,4},{4,5},{5,6},{6,7},{8,9},{9,10},{10,11},{11... | collective-permute-start | bytes 294920 | tf_op jit(solution)/shard_map/ppermute | solution.py:17
  22.3 0.6 collective-permute-done.3
  22.9 3.2 %collective-permute-done.2 = bf16[3,1,4,128,32]{3,4,2,1,0:T(8,128)(2,1)S(1)} collective-permute-done((bf16[3,1,4,128,32]{3,4,2,1,0:T(8,128)(2,1)S(1)}, bf16[3,1,4,128,32]{3,4,2,1,0:T(8,128)(2,1)S(1)}, u32[]{:S(2)}, u32[]{:S(2)}) %collective-permute-start.2) | collective-permute-done | bytes 98336 | tf_op jit(solution)/shard_map/ppermute | solution.py:17
  26.4 68.6 %all-gather = f32[32,64,32]{1,2,0:T(8,128)S(1)} all-gather(f32[1,64,32]{1,2,0:T(8,128)S(1)} %convolution_bitcast_fusion.3), channel_id=1, replica_groups=mesh['row'=4,'col'=8] {'row','col'}, dimensions={0}, use_global_device_ids=true | all-gather | bytes 270336 | tf_op jit(solution)/shard_map/all_gather | solution.py:51
  95.4 11.5 %scatter_custom_fusion = f32[256,32]{1,0:T(8,128)S(1)} fusion(s32[2048]{0:T(1024)S(1)} %compare_select_fusion, f32[2048,32]{1,0:T(8,128)S(1)} %bitcast.68, f32[]{:T(128)} %constant.48.clone.1), kind=kCustom, calls=%fused_computation.18 | custom fusion | flops 65536 | bytes 32772 | tf_op jit(solution)/shard_map/scatter-add | solution.py:47
  106.9 1.3 convolution_bitcast_fusion.1
  108.2 69.0 %all-reduce.2.cloned.1.call-done = f32[512,32]{0,1:T(8,128)} async-done(((f32[512,32]{0,1:T(8,128)}), f32[512,32]{0,1:T(8,128)}) %all-reduce.2.cloned.1.call-update) | async-done | bytes 65552 | tf_op jit(solution)/shard_map/psum | solution.py:54
  177.2 6.0 %all_gather.7 = f32[2048,32]{0,1:T(8,128)S(1)} all-gather(f32[512,32]{0,1:T(8,128)} %all-reduce.2.cloned.1.call-done), channel_id=1, replica_groups=mesh['row'=4,'col'=8] {'row'}, dimensions={0}, use_global_device_ids=true | all-gather | bytes 327680 | tf_op jit(solution)/shard_map/all_gather | solution.py:55
  183.5 0.6 gather_fusion.1
  184.6 2.2 %collective-permute-start.5 = (f32[1,1,4,128,32]{3,4,2,1,0:T(8,128)S(1)}, f32[1,1,4,128,32]{3,4,2,1,0:T(8,128)S(1)}, u32[]{:S(2)}, u32[]{:S(2)}) collective-permute-start(f32[1,1,4,128,32]{3,4,2,1,0:T(8,128)S(1)} %copy.40), channel_id=1, source_target_pairs={{0,8},{8,16},{16,24},{1,9},{9,17},{17,25},{2,10},{10,18},{18,26},{... | collective-permute-start | bytes 196616 | tf_op jit(solution)/shard_map/ppermute | solution.py:17
  186.8 1.3 collective-permute-start.4
  188.2 2.5 %collective-permute-done.4 = f32[1,1,4,128,32]{3,4,2,1,0:T(8,128)S(1)} collective-permute-done((f32[1,1,4,128,32]{3,4,2,1,0:T(8,128)S(1)}, f32[1,1,4,128,32]{3,4,2,1,0:T(8,128)S(1)}, u32[]{:S(2)}, u32[]{:S(2)}) %collective-permute-start.4) | collective-permute-done | bytes 65568 | tf_op jit(solution)/shard_map/ppermute | solution.py:19
  190.7 1.3 collective-permute-start.6
  192.0 4.6 %collective-permute-start.7 = (f32[3,1,4,128,32]{3,4,2,1,0:T(8,128)S(1)}, f32[3,1,4,128,32]{3,4,2,1,0:T(8,128)S(1)}, u32[]{:S(2)}, u32[]{:S(2)}) collective-permute-start(f32[3,1,4,128,32]{3,4,2,1,0:T(8,128)S(1)} %constant_dynamic-update-slice_fusion.1), channel_id=1, source_target_pairs={{0,1},{1,2},{2,3},{3,4},{4,5},{5,6},{6,7},{8,9},{9,10},{10,11},{11... | collective-permute-start | bytes 589832 | tf_op jit(solution)/shard_map/ppermute | solution.py:17
  196.6 1.8 collective-permute-done.6
  198.5 6.0 %collective-permute-done.7 = f32[3,1,4,128,32]{3,4,2,1,0:T(8,128)S(1)} collective-permute-done((f32[3,1,4,128,32]{3,4,2,1,0:T(8,128)S(1)}, f32[3,1,4,128,32]{3,4,2,1,0:T(8,128)S(1)}, u32[]{:S(2)}, u32[]{:S(2)}) %collective-permute-start.7) | collective-permute-done | bytes 196640 | tf_op jit(solution)/shard_map/ppermute | solution.py:17
  204.7 1.1 fusion.1
  (50 shorter events, 1.9 us)
Async XLA Ops:
  6.5 198.2 %copy-start = (bf16[512,1024]{1,0:T(8,128)(2,1)S(1)}, bf16[512,1024]{1,0:T(8,128)(2,1)}, u32[]{:S(2)}) copy-start(bf16[512,1024]{1,0:T(8,128)(2,1)} %param.8) | copy-start | bytes 3145732
  6.5 0.8 copy-start.7
  6.5 170.7 %all-reduce.2.cloned.1.call-start = ((), (), s32[]{:S(2)}) async-start(), calls=%async_computation | async-start | bytes 131072 | tf_op jit(solution)/shard_map/psum | solution.py:54
  8.1 4.4 %copy-start.3 = (bf16[512,32]{0,1:T(8,128)(2,1)S(1)}, bf16[512,32]{0,1:T(8,128)(2,1)}, u32[]{:S(2)}) copy-start(bf16[512,32]{0,1:T(8,128)(2,1)} %param.6) | copy-start | bytes 98308
  8.1 4.4 %copy-start.6 = (s32[2048]{0:T(1024)S(1)}, s32[2048]{0:T(1024)}, u32[]{:S(2)}) copy-start(s32[2048]{0:T(1024)} %param.10) | copy-start | bytes 24580
  8.7 17.5 %copy-start.1 = (f32[1024,64]{0,1:T(8,128)S(1)}, f32[1024,64]{0,1:T(8,128)}, u32[]{:S(2)}) copy-start(f32[1024,64]{0,1:T(8,128)} %param.9) | copy-start | bytes 786436
  8.8 3.9 %collective-permute-start = (bf16[1,1,4,128,32]{3,4,2,1,0:T(8,128)(2,1)S(1)}, bf16[1,1,4,128,32]{3,4,2,1,0:T(8,128)(2,1)S(1)}, u32[]{:S(2)}, u32[]{:S(2)}) collective-permute-start(bf16[1,1,4,128,32]{3,4,2,1,0:T(8,128)(2,1)S(1)} %bitcast_select_fusion), channel_id=1, source_target_pairs={{0,8},{8,16},{16,24},{1,9},{9,17},{17,25},{2,10},{10,18},{18,26},{... | collective-permute-start | bytes 98312 | tf_op jit(solution)/shard_map/ppermute | solution.py:17
  11.2 5.2 %collective-permute-start.1 = (bf16[1,1,4,128,32]{3,4,2,1,0:T(8,128)(2,1)S(1)}, bf16[1,1,4,128,32]{3,4,2,1,0:T(8,128)(2,1)S(1)}, u32[]{:S(2)}, u32[]{:S(2)}) collective-permute-start(bf16[1,1,4,128,32]{3,4,2,1,0:T(8,128)(2,1)S(1)} %bitcast_select_fusion), channel_id=1, source_target_pairs={{8,0},{16,8},{24,16},{9,1},{17,9},{25,17},{10,2},{18,10},{26,18},{... | collective-permute-start | bytes 98312 | tf_op jit(solution)/shard_map/ppermute | solution.py:19
  16.4 6.5 %collective-permute-start.3 = (bf16[3,1,4,128,32]{3,4,2,1,0:T(8,128)(2,1)S(1)}, bf16[3,1,4,128,32]{3,4,2,1,0:T(8,128)(2,1)S(1)}, u32[]{:S(2)}, u32[]{:S(2)}) collective-permute-start(bf16[3,1,4,128,32]{3,4,2,1,0:T(8,128)(2,1)S(1)} %pad_maximum_fusion), channel_id=1, source_target_pairs={{1,0},{2,1},{3,2},{4,3},{5,4},{6,5},{7,6},{9,8},{10,9},{11,10},{12... | collective-permute-start | bytes 294920 | tf_op jit(solution)/shard_map/ppermute | solution.py:19
  17.7 8.4 %collective-permute-start.2 = (bf16[3,1,4,128,32]{3,4,2,1,0:T(8,128)(2,1)S(1)}, bf16[3,1,4,128,32]{3,4,2,1,0:T(8,128)(2,1)S(1)}, u32[]{:S(2)}, u32[]{:S(2)}) collective-permute-start(bf16[3,1,4,128,32]{3,4,2,1,0:T(8,128)(2,1)S(1)} %pad_maximum_fusion), channel_id=1, source_target_pairs={{0,1},{1,2},{2,3},{3,4},{4,5},{5,6},{6,7},{8,9},{9,10},{10,11},{11... | collective-permute-start | bytes 294920 | tf_op jit(solution)/shard_map/ppermute | solution.py:17
  95.1 11.9 %copy-start.2 = (f32[512,256]{1,0:T(8,128)S(1)}, f32[512,256]{1,0:T(8,128)}, u32[]{:S(2)}) copy-start(f32[512,256]{1,0:T(8,128)} %param.11) | copy-start | bytes 1572868
  184.6 3.6 %collective-permute-start.5 = (f32[1,1,4,128,32]{3,4,2,1,0:T(8,128)S(1)}, f32[1,1,4,128,32]{3,4,2,1,0:T(8,128)S(1)}, u32[]{:S(2)}, u32[]{:S(2)}) collective-permute-start(f32[1,1,4,128,32]{3,4,2,1,0:T(8,128)S(1)} %copy.40), channel_id=1, source_target_pairs={{0,8},{8,16},{16,24},{1,9},{9,17},{17,25},{2,10},{10,18},{18,26},{... | collective-permute-start | bytes 196616 | tf_op jit(solution)/shard_map/ppermute | solution.py:17
  186.8 3.9 %collective-permute-start.4 = (f32[1,1,4,128,32]{3,4,2,1,0:T(8,128)S(1)}, f32[1,1,4,128,32]{3,4,2,1,0:T(8,128)S(1)}, u32[]{:S(2)}, u32[]{:S(2)}) collective-permute-start(f32[1,1,4,128,32]{3,4,2,1,0:T(8,128)S(1)} %copy.40), channel_id=1, source_target_pairs={{8,0},{16,8},{24,16},{9,1},{17,9},{25,17},{10,2},{18,10},{26,18},{... | collective-permute-start | bytes 196616 | tf_op jit(solution)/shard_map/ppermute | solution.py:19
  188.2 8.5 %copy-start.4 = (f32[1,1,4,128,32]{3,4,2,1,0:T(8,128)}, f32[1,1,4,128,32]{3,4,2,1,0:T(8,128)S(1)}, u32[]{:S(2)}) copy-start(f32[1,1,4,128,32]{3,4,2,1,0:T(8,128)S(1)} %collective-permute-done.5) | copy-start | bytes 196612
  190.7 5.9 %copy-start.5 = (f32[1,1,4,128,32]{3,4,2,1,0:T(8,128)}, f32[1,1,4,128,32]{3,4,2,1,0:T(8,128)S(1)}, u32[]{:S(2)}) copy-start(f32[1,1,4,128,32]{3,4,2,1,0:T(8,128)S(1)} %collective-permute-done.4) | copy-start | bytes 196612
  190.7 7.7 %collective-permute-start.6 = (f32[3,1,4,128,32]{3,4,2,1,0:T(8,128)S(1)}, f32[3,1,4,128,32]{3,4,2,1,0:T(8,128)S(1)}, u32[]{:S(2)}, u32[]{:S(2)}) collective-permute-start(f32[3,1,4,128,32]{3,4,2,1,0:T(8,128)S(1)} %constant_dynamic-update-slice_fusion.1), channel_id=1, source_target_pairs={{1,0},{2,1},{3,2},{4,3},{5,4},{6,5},{7,6},{9,8},{10,9},{11,10},{12... | collective-permute-start | bytes 589832 | tf_op jit(solution)/shard_map/ppermute | solution.py:19
  192.0 12.4 %collective-permute-start.7 = (f32[3,1,4,128,32]{3,4,2,1,0:T(8,128)S(1)}, f32[3,1,4,128,32]{3,4,2,1,0:T(8,128)S(1)}, u32[]{:S(2)}, u32[]{:S(2)}) collective-permute-start(f32[3,1,4,128,32]{3,4,2,1,0:T(8,128)S(1)} %constant_dynamic-update-slice_fusion.1), channel_id=1, source_target_pairs={{0,1},{1,2},{2,3},{3,4},{4,5},{5,6},{6,7},{8,9},{9,10},{10,11},{11... | collective-permute-start | bytes 589832 | tf_op jit(solution)/shard_map/ppermute | solution.py:17
  198.5 6.0 %slice-start = ((f32[1,1,4,128,32]{3,4,2,1,0:T(8,128)}), f32[1,1,1,128,32]{3,4,2,1,0:T(8,128)S(1)}, s32[]{:S(2)}) async-start(f32[1,1,4,128,32]{3,4,2,1,0:T(8,128)} %copy-done.4), calls=%async_computation.1 | async-start | bytes 32768 | tf_op jit(solution)/shard_map/slice | solution.py:64
  198.5 6.0 %slice-start.1 = ((f32[1,1,4,128,32]{3,4,2,1,0:T(8,128)}), f32[1,1,1,128,32]{3,4,2,1,0:T(8,128)S(1)}, s32[]{:S(2)}) async-start(f32[1,1,4,128,32]{3,4,2,1,0:T(8,128)} %copy-done.5), calls=%async_computation.2 | async-start | bytes 32768 | tf_op jit(solution)/shard_map/slice | solution.py:64
Sparse Core Ops, SparseCore 0:
  108.3 68.8 all-reduce.1
where the time goes:
time: 213 us
  waiting for transfers between devices  87 us (41%)
  blocking collectives  74.6 us (35%)
  starting transfers between devices  18.9 us (9%)
  between operations  13.7 us (6%)
  other arithmetic  12.5 us (6%)
  matrix products  3.2 us (2%)
  local copies, waits for them, and re-layouts  2.73 us (1%)
    psum x1, waiting for transfers between devices, shards(): row_total = lax.psum(product, 'col')  69 us
    all_gather x1, blocking collectives, shards(): lax.all_gather(a, ('row', 'col'), axis=0, tiled=True)  68.6 us
    ppermute x4, starting transfers between devices, extended(): lax.ppermute(tail, axis, [(i, (i + 1) % count) for i in range(ends)])  13.8 us
    scatter-add x1, other arithmetic, add_piece(): return carry.at[target].add(piece, mode='drop')  11.5 us
    ppermute x4, waiting for transfers between devices, extended(): lax.ppermute(tail, axis, [(i, (i + 1) % count) for i in range(ends)])  9.2 us
    ppermute x4, waiting for transfers between devices, extended(): lax.ppermute(head, axis, [((i + 1) % count, i) for i in range(ends)])  8.78 us
    all_gather x1, blocking collectives, shards(): whole_coarse = lax.all_gather(row_total, 'row', axis=0, tiled=True)  5.98 us
    ppermute x4, starting transfers between devices, extended(): lax.ppermute(head, axis, [((i + 1) % count, i) for i in range(ends)])  5.17 us
  transfers between devices with their start and end apart: 9, of which 7 were waited for; matrix products, arithmetic and copies ran while one was open for 0% of the time, Pallas kernels for 0%

commit v1 on v0

v1 whole, which is shorter than its diff:
```python
import functools

import jax
import jax.numpy as jnp
from jax import lax
from jax.experimental import pallas as pl
from jax.experimental.pallas import tpu as pltpu
from jax.sharding import PartitionSpec as P

MESH = pl.DeviceIdType.MESH
BLK = 128
LANES = 128
UNROLL = 16
NT = (((1,), (1,)), ((), ()))
NN = (((1,), (0,)), ((), ()))
F32 = jnp.float32
BF16 = jnp.bfloat16


def matmul(a, b, dims):
    return lax.dot_general(a, b, dims, preferred_element_type=F32)


def split(x):
    hi = x.astype(BF16)
    return hi, (x - hi.astype(F32)).astype(BF16)


def loop(start, stop, body):
    if stop - start <= UNROLL:
        for i in range(start, stop):
            body(i)
    else:
        def step(i, carry):
            body(i)
            return carry

        lax.fori_loop(start, stop, step, 0)


def flipped(index, k, count):
    out = index
    bit = 1
    while bit < count:
        kbit = (k // bit) % 2
        out = out + kbit * bit * (1 - 2 * ((index // bit) % 2))
        bit *= 2
    return out


def lane_low(shape):
    return lax.broadcasted_iota(jnp.int32, shape, len(shape) - 1) < LANES // 2


def half_roll(x):
    return pltpu.roll(x, LANES // 2, 1)


def kernel(
    nrow,
    ncol,
    res_ref,
    ib_ref,
    linv_hbm,
    basis_hbm,
    slots_ref,
    coarse_hbm,
    out_ref,
    outgoing,
    incoming,
    linv,
    basis,
    basis2,
    coarse,
    coarse_hi,
    coarse_lo,
    hot_in,
    hot_out,
    gathered,
    gathered2,
    pieces,
    received,
    solved,
    returning,
    returned,
    load_sem,
    halo_send,
    halo_recv,
    back_send,
    back_recv,
    ag1_send,
    ag1_recv,
    rs_send,
    rs_recv,
    ag2_send,
    ag2_recv,
):
    r = lax.axis_index("row")
    c = lax.axis_index("col")
    me = r * ncol + c
    rhs = res_ref.shape[0]
    own = res_ref.shape[1]
    half = rhs // 2
    ndev = nrow * ncol
    rows, width = coarse.shape
    total = slots_ref.shape[1]

    def col_peer(k):
        return (r, flipped(c, k, ncol))

    def row_peer(j):
        return (lax.rem(r + j, nrow), c)

    barrier = pltpu.get_barrier_semaphore()
    loop(1, ncol, lambda k: pl.semaphore_signal(barrier, inc=1, device_id=col_peer(ncol - k), device_id_type=MESH))
    loop(1, nrow, lambda j: pl.semaphore_signal(barrier, inc=1, device_id=row_peer(j), device_id_type=MESH))

    loads = [
        pltpu.make_async_copy(basis_hbm, basis, load_sem.at[0]),
        pltpu.make_async_copy(coarse_hbm, coarse, load_sem.at[1]),
        pltpu.make_async_copy(linv_hbm, linv, load_sem.at[2]),
    ]
    for load in loads:
        load.start()

    exists = [r < nrow - 1, r > 0, c < ncol - 1, c > 0]
    target = [(r + 1, c), (r - 1, c), (r, c + 1), (r, c - 1)]
    opposite = [1, 0, 3, 2]
    blocks = [res_ref[:, b * BLK:(b + 1) * BLK] for b in range(own // BLK)]
    for d in range(4):
        index = ib_ref[0, d]
        value = blocks[0]
        for b in range(1, len(blocks)):
            value = jnp.where(index == b, blocks[b], value)
        outgoing[d] = value

        @pl.when(jnp.logical_not(exists[opposite[d]]))
        def _():
            incoming[d] = jnp.zeros_like(incoming[d])

        @pl.when(jnp.logical_not(exists[d]))
        def _():
            returned[d] = jnp.zeros_like(returned[d])

    def halo(d):
        return pltpu.make_async_remote_copy(
            src_ref=outgoing.at[d], dst_ref=incoming.at[d],
            send_sem=halo_send.at[d], recv_sem=halo_recv.at[d],
            device_id=target[d], device_id_type=MESH)

    def back(d):
        return pltpu.make_async_remote_copy(
            src_ref=returning.at[d], dst_ref=returned.at[d],
            send_sem=back_send.at[d], recv_sem=back_recv.at[d],
            device_id=target[opposite[d]], device_id_type=MESH)

    pl.semaphore_wait(barrier, ncol + nrow - 2)
    for d in range(4):
        @pl.when(exists[d])
        def _():
            halo(d).start()

    loads[0].wait()
    nev = basis.shape[0]
    b_hi, b_lo = split(basis[...])
    basis2[:nev] = b_hi
    basis2[nev:] = b_lo
    partial = matmul(res_ref[...], basis2[:, :own], NT)

    for d in range(4):
        @pl.when(exists[opposite[d]])
        def _():
            halo(d).wait_recv()

    inc = jnp.concatenate([incoming[d] for d in range(4)], axis=1)
    partial = partial + matmul(inc, basis2[:, own:], NT)
    partial = partial + half_roll(partial)
    low = lane_low((half, LANES))
    gathered[me] = jnp.where(low, partial[:half], partial[half:])

    def spread(buf, send, recv):
        def to_col(k):
            return pltpu.make_async_remote_copy(
                src_ref=buf.at[me], dst_ref=buf.at[me],
                send_sem=send.at[k, 0], recv_sem=recv.at[me],
                device_id=col_peer(k), device_id_type=MESH)

        def to_row(k, j):
            slot = r * ncol + flipped(c, k, ncol)
            return pltpu.make_async_remote_copy(
                src_ref=buf.at[slot], dst_ref=buf.at[slot],
                send_sem=send.at[k, j], recv_sem=recv.at[slot],
                device_id=row_peer(j), device_id_type=MESH)

        def arrival(slot):
            pltpu.make_async_remote_copy(
                src_ref=buf.at[slot], dst_ref=buf.at[slot],
                send_sem=send.at[0, 0], recv_sem=recv.at[slot],
                device_id=row_peer(1), device_id_type=MESH).wait_recv()

        def start():
            loop(1, ncol, lambda i: to_col(ncol - i).start())
            for j in range(1, nrow):
                to_row(0, j).start()

        def relay(first, last):
            def one(k):
                arrival(r * ncol + flipped(c, k, ncol))
                for j in range(1, nrow):
                    to_row(k, j).start()

            loop(first, last, one)

        def finish():
            def one(k):
                for j in range(1, nrow):
                    arrival(lax.rem(r + j, nrow) * ncol + flipped(c, k, ncol))

            loop(0, ncol, one)

        def drain():
            def one(k):
                for j in range(1, nrow):
                    to_row(k, j).wait_send()

            loop(0, ncol, one)
            loop(1, ncol, lambda k: to_col(k).wait_send())

        return start, relay, finish, drain

    def unpacked(buf):
        def one(p):
            a, b = buf[2 * p], buf[2 * p + 1]
            top = jnp.where(low, a, half_roll(b))
            bot = jnp.where(low, half_roll(a), b)
            t_hi, t_lo = split(top)
            b_hi, b_lo = split(bot)
            lanes = pl.ds(p * LANES if isinstance(p, int) else pl.multiple_of(p * LANES, LANES), LANES)
            gathered2[0 * half:1 * half, lanes] = t_hi
            gathered2[1 * half:2 * half, lanes] = b_hi
            gathered2[2 * half:3 * half, lanes] = t_lo
            gathered2[3 * half:4 * half, lanes] = b_lo

        loop(0, ndev // 2, one)

    start1, relay1, finish1, drain1 = spread(gathered, ag1_send, ag1_recv)
    start1()

    loads[2].wait()
    local = jnp.concatenate([res_ref[...], inc], axis=1)
    out_ref[...] = matmul(local, linv[...], NT)
    relay1(1, ncol // 2)
    chunk = 2 * LANES

    def build_in(i):
        lanes = pl.ds(i * chunk if isinstance(i, int) else pl.multiple_of(i * chunk, chunk), chunk)
        slot = slots_ref[:, lanes] - c * width
        place = lax.broadcasted_iota(jnp.int32, (width, chunk), 0)
        hot_in[:, lanes] = jnp.where(place == slot, 1.0, 0.0).astype(BF16)

    loop(0, total // chunk, build_in)
    relay1(ncol // 2, ncol)
    loads[1].wait()
    a_hi, a_lo = split(coarse[...])
    coarse_hi[...] = a_hi
    coarse_lo[...] = a_lo
    finish1()

    unpacked(gathered)
    depth = min(total, 2048)
    column = matmul(gathered2[:, :depth], hot_in[:, :depth], NT)
    if total > depth:
        def more(i, acc):
            lanes = pl.ds(pl.multiple_of(i * depth, depth), depth)
            return acc + matmul(gathered2[:, lanes], hot_in[:, lanes], NT)

        column = lax.fori_loop(1, total // depth, more, column)
    column_hi, column_lo = split(column[:rhs] + column[rhs:])
    column2 = jnp.concatenate([column_hi, column_lo], axis=0)
    span = 2 * LANES

    def product(i):
        at = pl.ds(i * span if isinstance(i, int) else pl.multiple_of(i * span, span), span)
        part = matmul(column2, coarse_hi[at], NT) + matmul(column2, coarse_lo[at], NT)
        part = part[:rhs] + part[rhs:]
        for q in range(span // LANES):
            top = part[:half, q * LANES:(q + 1) * LANES]
            bot = part[half:, q * LANES:(q + 1) * LANES]
            pieces[(span // LANES * i + q) * 2] = jnp.where(low, top, half_roll(bot))
            pieces[(span // LANES * i + q) * 2 + 1] = jnp.where(low, half_roll(top), bot)

    loop(0, rows // span, product)

    def reduce(k):
        peer = flipped(c, k, ncol)
        return pltpu.make_async_remote_copy(
            src_ref=pieces.at[peer], dst_ref=received.at[c],
            send_sem=rs_send.at[k], recv_sem=rs_recv.at[c],
            device_id=(r, peer), device_id_type=MESH)

    def reduce_arrival(k):
        peer = flipped(c, k, ncol)
        pltpu.make_async_remote_copy(
            src_ref=pieces.at[peer], dst_ref=received.at[peer],
            send_sem=rs_send.at[k], recv_sem=rs_recv.at[peer],
            device_id=(r, peer), device_id_type=MESH).wait_recv()

    loop(1, ncol, lambda i: reduce(ncol - i).start())

    at = pl.ds(pl.multiple_of((me // 2) * LANES, LANES), LANES)
    mine = jnp.broadcast_to(slots_ref[:, at], (8, LANES))
    swapped = half_roll(mine)
    low8 = lane_low((8, LANES))
    mine = jnp.where(lax.rem(me, 2) == 0, jnp.where(low8, mine, swapped), jnp.where(low8, swapped, mine))[:1]
    tall = 4 * LANES

    def build_out(i):
        at = pl.ds(i * tall if isinstance(i, int) else pl.multiple_of(i * tall, tall), tall)
        place = lax.broadcasted_iota(jnp.int32, (tall, LANES), 0) + i * tall
        hot_out[at] = jnp.where(place == mine, 1.0, 0.0).astype(BF16)

    loop(0, total // tall, build_out)

    loop(1, ncol, reduce_arrival)
    summed = pieces[c]
    if ncol - 1 <= UNROLL:
        for k in range(1, ncol):
            summed = summed + received[flipped(c, k, ncol)]
    else:
        summed = lax.fori_loop(1, ncol, lambda k, acc: acc + received[flipped(c, k, ncol)], summed)
    solved[me] = summed

    start2, relay2, finish2, drain2 = spread(solved, ag2_send, ag2_recv)
    start2()
    relay2(1, ncol)
    finish2()
    unpacked(solved)
    picked = matmul(gathered2[:, :depth], hot_out[:depth], NN)
    if total > depth:
        def again(i, acc):
            at = pl.ds(pl.multiple_of(i * depth, depth), depth)
            return acc + matmul(gathered2[:, at], hot_out[at], NN)

        picked = lax.fori_loop(1, total // depth, again, picked)
    picked = picked.astype(BF16)

    outer = matmul(picked, basis2[:, own:], NN)
    outer = outer[:rhs] + outer[rhs:]
    for d in range(4):
        returning[d] = outer[:, d * BLK:(d + 1) * BLK]

        @pl.when(exists[opposite[d]])
        def _():
            back(d).start()

    inner = matmul(picked, basis2[:, :own], NN)
    out_ref[...] = out_ref[...] + inner[:rhs] + inner[rhs:]
    for d in range(4):
        @pl.when(exists[d])
        def _():
            back(d).wait_recv()

    for b in range(own // BLK):
        value = out_ref[:, b * BLK:(b + 1) * BLK]
        for d in range(4):
            value = value + jnp.where(ib_ref[0, d] == b, returned[d], 0.0)
        out_ref[:, b * BLK:(b + 1) * BLK] = value

    drain1()
    drain2()
    loop(1, ncol, lambda k: reduce(k).wait_send())
    for d in range(4):
        @pl.when(exists[d])
        def _():
            halo(d).wait_send()

        @pl.when(exists[opposite[d]])
        def _():
            back(d).wait_send()


def shards(nrow, ncol, residuals, intersect_blocks, local_inverse, coarse_basis, coarse_slots, coarse_inverse):
    own, rhs = residuals.shape
    loc, nev = coarse_basis.shape
    rows, width = coarse_inverse.shape
    total = coarse_slots.shape[0]
    ndev = nrow * ncol
    assert 2 * nev == LANES and rows == ncol * nev and loc == own + 4 * BLK and own % BLK == 0
    packed = (rhs // 2, LANES)
    vmem = pl.BlockSpec(memory_space=pltpu.VMEM)
    hbm = pl.BlockSpec(memory_space=pl.ANY)
    dma = pltpu.SemaphoreType.DMA
    out = pl.pallas_call(
        functools.partial(kernel, nrow, ncol),
        name="schwarz",
        out_shape=jax.ShapeDtypeStruct((rhs, own), F32),
        in_specs=[vmem, pl.BlockSpec(memory_space=pltpu.SMEM), hbm, hbm, vmem, hbm],
        out_specs=vmem,
        scratch_shapes=[
            pltpu.VMEM((4, rhs, BLK), BF16),
            pltpu.VMEM((4, rhs, BLK), BF16),
            pltpu.VMEM((own, loc), BF16),
            pltpu.VMEM((nev, loc), F32),
            pltpu.VMEM((2 * nev, loc), BF16),
            pltpu.VMEM((rows, width), F32),
            pltpu.VMEM((rows, width), BF16),
            pltpu.VMEM((rows, width), BF16),
            pltpu.VMEM((width, total), BF16),
            pltpu.VMEM((total, LANES), BF16),
            pltpu.VMEM((ndev,) + packed, F32),
            pltpu.VMEM((2 * rhs, total), BF16),
            pltpu.VMEM((ncol,) + packed, F32),
            pltpu.VMEM((ncol,) + packed, F32),
            pltpu.VMEM((ndev,) + packed, F32),
            pltpu.VMEM((4, rhs, BLK), F32),
            pltpu.VMEM((4, rhs, BLK), F32),
            dma((3,)),
            dma((4,)),
            dma((4,)),
            dma((4,)),
            dma((4,)),
            dma((ncol, nrow)),
            dma((ndev,)),
            dma((ncol,)),
            dma((ncol,)),
            dma((ncol, nrow)),
            dma((ndev,)),
        ],
        compiler_params=pltpu.CompilerParams(collective_id=0, has_side_effects=True),
    )(
        residuals.T,
        intersect_blocks,
        local_inverse,
        coarse_basis.T,
        coarse_slots.reshape(1, total),
        coarse_inverse,
    )
    return out.T


def solution(mesh):
    placed = (
        P(("row", "col"), None),
        P(("row", "col"), None),
        P(("row", "col"), None),
        P(("row", "col"), None),
        P(),
        P("row", "col"),
    )
    return jax.shard_map(
        functools.partial(shards, mesh.shape["row"], mesh.shape["col"]),
        mesh=mesh, in_specs=placed, out_specs=P(("row", "col"), None), check_vma=False,
    )
```

time: 213 us -> 36.2 us (0.17)
  waiting for transfers between devices: 87 us -> 0 us
  blocking collectives: 74.6 us -> 0 us
  Pallas kernels: 0 us -> 34.4 us
  starting transfers between devices: 18.9 us -> 0 us
  between operations: 13.7 us -> 0.01 us
  other arithmetic: 12.5 us -> 0 us
  matrix products: 3.2 us -> 0 us
    all_gather x2 -> x0, blocking collectives: 74.6 us -> none  [the longest x1 68.6 us: shards(): lax.all_gather(a, ('row', 'col'), axis=0, tiled=True)]
    psum x1 -> x0, waiting for transfers between devices: 69 us -> none  [shards(): row_total = lax.psum(product, 'col')]
    pallas_call x0 -> x1, Pallas kernels: none -> 34.4 us  [shards(): pl.pallas_call(functools.partial(kernel, nrow, ncol), name='schwarz', out...]
    ppermute x8 -> x0, starting transfers between devices: 18.9 us -> none  [the longest x4 13.8 us: extended(): lax.ppermute(tail, axis, [(i, (i + 1) % count) for i in range(ends)])]
    ppermute x8 -> x0, waiting for transfers between devices: 18 us -> none  [the longest x4 9.2 us: extended(): lax.ppermute(tail, axis, [(i, (i + 1) % count) for i in range(ends)])]
    scatter-add x1 -> x0, other arithmetic: 11.5 us -> none  [add_piece(): return carry.at[target].add(piece, mode='drop')]
    dot_general x5 -> x0, matrix products: 3.2 us -> none  [the longest x1 1.26 us: shards(): jnp.dot(coarse_inverse, column_part, precision=lax.Precision.HIGHEST)]
  transfers between devices with their start and end apart: 9 -> 0, of which waited for: 7 -> 0; matrix products, arithmetic and copies ran while one was open for 0% -> 0% of each run, Pallas kernels for 0% -> 0%
where the time goes in v1:
time: 36.2 us; the launch traced here: 35.9 us
  Pallas kernels  34.4 us (95%)
  local copies, waits for them, and re-layouts  1.47 us (4%)
    pallas_call x1, Pallas kernels, shards(): pl.pallas_call(functools.partial(kernel, nrow, ncol), name='schwarz', out...  34.4 us
    unnamed x1, local copies, waits for them, and re-layouts  1.47 us

profile of v1, /device:TPU:0, one launch (start us, length us, event | category | flops | bytes accessed | tf_op | source)
XLA Modules:
  0.0 35.9 jit_solution(4290727050819198816)
XLA Ops:
  0.0 34.4 %schwarz.1 = f32[32,512]{1,0:T(8,128)} custom-call(bf16[32,512]{1,0:T(8,128)(2,1)} %bitcast.6, s32[1,4]{1,0:T(1,128)} %ib_ref.1, bf16[512,1024]{1,0:T(8,128)(2,1)} %linv_hbm.1, f32[64,1024]{1,0:T(8,128)} %bitcast.4, s32[1,2048]{1,0:T(1,128)} %bitcast.7, f32[512,256]{1,0:T(8,128)} %coarse_hbm.1), custom_call_target="tpu_custom_call" | custom-call | tf_op jit(solution)/shard_map/schwarz/pallas_call | solution.py:393
  34.5 1.5 %copy.8 = f32[512,32]{0,1:T(8,128)} copy(f32[512,32]{0,1:T(8,128)} %bitcast.5) | data formatting | bytes 131072

commit v2 on v1

--- a/solution.py
+++ b/solution.py
@@ -59,13 +59,16 @@
 def kernel(
     nrow,
     ncol,
+    res_hbm,
+    ib_hbm,
+    linv_hbm,
+    basis_hbm,
+    slots_hbm,
+    coarse_hbm,
+    out_ref,
     res_ref,
     ib_ref,
-    linv_hbm,
-    basis_hbm,
     slots_ref,
-    coarse_hbm,
-    out_ref,
     outgoing,
     incoming,
     linv,
@@ -81,13 +84,14 @@
     pieces,
     received,
     solved,
-    returning,
-    returned,
+    lent,
+    wide_hi,
+    wide_lo,
     load_sem,
     halo_send,
     halo_recv,
-    back_send,
-    back_recv,
+    lend_send,
+    lend_recv,
     ag1_send,
     ag1_recv,
     rs_send,
@@ -119,9 +123,14 @@
         pltpu.make_async_copy(basis_hbm, basis, load_sem.at[0]),
         pltpu.make_async_copy(coarse_hbm, coarse, load_sem.at[1]),
         pltpu.make_async_copy(linv_hbm, linv, load_sem.at[2]),
+        pltpu.make_async_copy(res_hbm, res_ref, load_sem.at[3]),
+        pltpu.make_async_copy(ib_hbm, ib_ref, load_sem.at[4]),
+        pltpu.make_async_copy(slots_hbm, slots_ref, load_sem.at[5]),
     ]
-    for load in loads:
+    for load in loads[3:] + loads[:3]:
         load.start()
+    loads[4].wait()
+    loads[3].wait()
 
     exists = [r < nrow - 1, r > 0, c < ncol - 1, c > 0]
     target = [(r + 1, c), (r - 1, c), (r, c + 1), (r, c - 1)]
@@ -140,7 +149,7 @@
 
         @pl.when(jnp.logical_not(exists[d]))
         def _():
-            returned[d] = jnp.zeros_like(returned[d])
+            lent[d] = jnp.zeros_like(lent[d])
 
     def halo(d):
         return pltpu.make_async_remote_copy(
@@ -148,10 +157,10 @@
             send_sem=halo_send.at[d], recv_sem=halo_recv.at[d],
             device_id=target[d], device_id_type=MESH)
 
-    def back(d):
+    def lend(d):
         return pltpu.make_async_remote_copy(
-            src_ref=returning.at[d], dst_ref=returned.at[d],
-            send_sem=back_send.at[d], recv_sem=back_recv.at[d],
+            src_ref=basis.at[:, pl.ds(own + d * BLK, BLK)], dst_ref=lent.at[d],
+            send_sem=lend_send.at[d], recv_sem=lend_recv.at[d],
             device_id=target[opposite[d]], device_id_type=MESH)
 
     pl.semaphore_wait(barrier, ncol + nrow - 2)
@@ -245,12 +254,17 @@
 
     start1, relay1, finish1, drain1 = spread(gathered, ag1_send, ag1_recv)
     start1()
+    for d in range(4):
+        @pl.when(exists[opposite[d]])
+        def _():
+            lend(d).start()
 
     loads[2].wait()
     local = jnp.concatenate([res_ref[...], inc], axis=1)
     out_ref[...] = matmul(local, linv[...], NT)
     relay1(1, ncol // 2)
     chunk = 2 * LANES
+    loads[5].wait()
 
     def build_in(i):
         lanes = pl.ds(i * chunk if isinstance(i, int) else pl.multiple_of(i * chunk, chunk), chunk)
@@ -307,19 +321,45 @@
 
     loop(1, ncol, lambda i: reduce(ncol - i).start())
 
-    at = pl.ds(pl.multiple_of((me // 2) * LANES, LANES), LANES)
-    mine = jnp.broadcast_to(slots_ref[:, at], (8, LANES))
-    swapped = half_roll(mine)
     low8 = lane_low((8, LANES))
-    mine = jnp.where(lax.rem(me, 2) == 0, jnp.where(low8, mine, swapped), jnp.where(low8, swapped, mine))[:1]
+
+    def slots_of(device):
+        device = jnp.clip(device, 0, ndev - 1)
+        at = pl.ds(pl.multiple_of((device // 2) * LANES, LANES), LANES)
+        pair = jnp.broadcast_to(slots_ref[:, at], (8, LANES))
+        swapped = half_roll(pair)
+        return jnp.where(lax.rem(device, 2) == 0, jnp.where(low8, pair, swapped), jnp.where(low8, swapped, pair))
+
+    mine = [
+        jnp.where(low8, slots_of(me), slots_of(me + ncol))[:1],
+        jnp.where(low8, slots_of(me - ncol), slots_of(me + 1))[:1],
+        jnp.where(low8, slots_of(me - 1), -1)[:1],
+    ]
     tall = 4 * LANES
 
     def build_out(i):
         at = pl.ds(i * tall if isinstance(i, int) else pl.multiple_of(i * tall, tall), tall)
         place = lax.broadcasted_iota(jnp.int32, (tall, LANES), 0) + i * tall
-        hot_out[at] = jnp.where(place == mine, 1.0, 0.0).astype(BF16)
+        for q in range(3):
+            hot_out[at, q * LANES:(q + 1) * LANES] = jnp.where(place == mine[q], 1.0, 0.0).astype(BF16)
 
     loop(0, total // tall, build_out)
+
+    wide_hi[:nev] = basis2[:nev, :own]
+    wide_lo[:nev] = basis2[nev:, :own]
+    wide_hi[5 * nev:] = jnp.zeros_like(wide_hi[5 * nev:])
+    wide_lo[5 * nev:] = jnp.zeros_like(wide_lo[5 * nev:])
+    for d in range(4):
+        @pl.when(exists[d])
+        def _():
+            lend(d).wait_recv()
+
+        l_hi, l_lo = split(lent[d])
+        for b in range(own // BLK):
+            here = ib_ref[0, d] == b
+            at = slice((d + 1) * nev, (d + 2) * nev), slice(b * BLK, (b + 1) * BLK)
+            wide_hi[at] = jnp.where(here, l_hi, jnp.zeros_like(l_hi))
+            wide_lo[at] = jnp.where(here, l_lo, jnp.zeros_like(l_lo))
 
     loop(1, ncol, reduce_arrival)
     summed = pieces[c]
@@ -344,27 +384,8 @@
         picked = lax.fori_loop(1, total // depth, again, picked)
     picked = picked.astype(BF16)
 
-    outer = matmul(picked, basis2[:, own:], NN)
-    outer = outer[:rhs] + outer[rhs:]
-    for d in range(4):
-        returning[d] = outer[:, d * BLK:(d + 1) * BLK]
-
-        @pl.when(exists[opposite[d]])
-        def _():
-            back(d).start()
-
-    inner = matmul(picked, basis2[:, :own], NN)
+    inner = matmul(picked, wide_hi[...], NN) + matmul(picked, wide_lo[...], NN)
     out_ref[...] = out_ref[...] + inner[:rhs] + inner[rhs:]
-    for d in range(4):
-        @pl.when(exists[d])
-        def _():
-            back(d).wait_recv()
-
-    for b in range(own // BLK):
-        value = out_ref[:, b * BLK:(b + 1) * BLK]
-        for d in range(4):
-            value = value + jnp.where(ib_ref[0, d] == b, returned[d], 0.0)
-        out_ref[:, b * BLK:(b + 1) * BLK] = value
 
     drain1()
     drain2()
@@ -376,7 +397,7 @@
 
         @pl.when(exists[opposite[d]])
         def _():
-            back(d).wait_send()
+            lend(d).wait_send()
 
 
 def shards(nrow, ncol, residuals, intersect_blocks, local_inverse, coarse_basis, coarse_slots, coarse_inverse):
@@ -393,10 +414,13 @@
     out = pl.pallas_call(
         functools.partial(kernel, nrow, ncol),
         name="schwarz",
-        out_shape=jax.ShapeDtypeStruct((rhs, own), F32),
-        in_specs=[vmem, pl.BlockSpec(memory_space=pltpu.SMEM), hbm, hbm, vmem, hbm],
+        out_shape=pltpu.VMEM((rhs, own), F32),
+        in_specs=[hbm] * 6,
         out_specs=vmem,
         scratch_shapes=[
+            pltpu.VMEM((rhs, own), BF16),
+            pltpu.SMEM(intersect_blocks.shape, jnp.int32),
+            pltpu.VMEM((1, total), jnp.int32),
             pltpu.VMEM((4, rhs, BLK), BF16),
             pltpu.VMEM((4, rhs, BLK), BF16),
             pltpu.VMEM((own, loc), BF16),
@@ -406,15 +430,16 @@
             pltpu.VMEM((rows, width), BF16),
             pltpu.VMEM((rows, width), BF16),
             pltpu.VMEM((width, total), BF16),
-            pltpu.VMEM((total, LANES), BF16),
+            pltpu.VMEM((total, 3 * LANES), BF16),
             pltpu.VMEM((ndev,) + packed, F32),
             pltpu.VMEM((2 * rhs, total), BF16),
             pltpu.VMEM((ncol,) + packed, F32),
             pltpu.VMEM((ncol,) + packed, F32),
             pltpu.VMEM((ndev,) + packed, F32),
-            pltpu.VMEM((4, rhs, BLK), F32),
-            pltpu.VMEM((4, rhs, BLK), F32),
-            dma((3,)),
+            pltpu.VMEM((4, nev, BLK), F32),
+            pltpu.VMEM((6 * nev, own), BF16),
+            pltpu.VMEM((6 * nev, own), BF16),
+            dma((6,)),
             dma((4,)),
             dma((4,)),
             dma((4,)),

time: 36.2 us -> 31.2 us (0.86)
  Pallas kernels: 34.4 us -> 30.5 us
  local copies, waits for them, and re-layouts: 1.47 us -> 0.63 us
    pallas_call x1, Pallas kernels: 34.4 us -> 30.5 us  [shards(): pl.pallas_call(functools.partial(kernel, nrow, ncol), name='schwarz', out...]
    unnamed x1, local copies, waits for them, and re-layouts: 1.47 us -> 0.63 us
where the time goes in v2:
time: 31.2 us; the launch traced here: 31.1 us
  Pallas kernels  30.5 us (98%)
  local copies, waits for them, and re-layouts  0.63 us (2%)
    pallas_call x1, Pallas kernels, shards(): pl.pallas_call(functools.partial(kernel, nrow, ncol), name='schwarz', out...  30.5 us
    unnamed x1, local copies, waits for them, and re-layouts  0.63 us

profile of v2, /device:TPU:0, one launch (start us, length us, event | category | flops | bytes accessed | tf_op | source)
XLA Modules:
  0.0 31.1 jit_solution(13190503772418095264)
XLA Ops:
  0.0 30.5 %schwarz.1 = f32[32,512]{1,0:T(8,128)S(1)} custom-call(bf16[32,512]{1,0:T(8,128)(2,1)} %bitcast.6, s32[1,4]{1,0:T(1,128)} %ib_hbm.1, bf16[512,1024]{1,0:T(8,128)(2,1)} %linv_hbm.1, f32[64,1024]{1,0:T(8,128)} %bitcast.5, s32[1,2048]{1,0:T(1,128)} %bitcast.7, f32[512,256]{1,0:T(8,128)} %coarse_hbm.1), custom_call_target="tpu_custom_call" | custom-call | tf_op jit(solution)/shard_map/schwarz/pallas_call | solution.py:414
  30.5 0.6 %copy.8 = f32[512,32]{0,1:T(8,128)} copy(f32[512,32]{0,1:T(8,128)S(1)} %bitcast.4) | data formatting | bytes 131072

commit v3 on v2

--- a/solution.py
+++ b/solution.py
@@ -11,6 +11,7 @@
 BLK = 128
 LANES = 128
 UNROLL = 16
+FAR_NUM, FAR_DEN = 3, 4
 NT = (((1,), (1,)), ((), ()))
 NN = (((1,), (0,)), ((), ()))
 F32 = jnp.float32
@@ -94,10 +95,12 @@
     lend_recv,
     ag1_send,
     ag1_recv,
+    ag1_rest,
     rs_send,
     rs_recv,
     ag2_send,
     ag2_recv,
+    ag2_rest,
 ):
     r = lax.axis_index("row")
     c = lax.axis_index("col")
@@ -187,53 +190,69 @@
     low = lane_low((half, LANES))
     gathered[me] = jnp.where(low, partial[:half], partial[half:])
 
-    def spread(buf, send, recv):
-        def to_col(k):
+    def spread(buf, send, recv, rest, far):
+        pairs = nrow // 2
+        partner = r + 1 - 2 * lax.rem(r, 2)
+        singles = ncol - 1 + (pairs - 1) * (ncol - far)
+
+        def copy(slot, sem, device):
             return pltpu.make_async_remote_copy(
-                src_ref=buf.at[me], dst_ref=buf.at[me],
-                send_sem=send.at[k, 0], recv_sem=recv.at[me],
-                device_id=col_peer(k), device_id_type=MESH)
-
-        def to_row(k, j):
-            slot = r * ncol + flipped(c, k, ncol)
-            return pltpu.make_async_remote_copy(
-                src_ref=buf.at[slot], dst_ref=buf.at[slot],
-                send_sem=send.at[k, j], recv_sem=recv.at[slot],
-                device_id=row_peer(j), device_id_type=MESH)
-
-        def arrival(slot):
-            pltpu.make_async_remote_copy(
-                src_ref=buf.at[slot], dst_ref=buf.at[slot],
-                send_sem=send.at[0, 0], recv_sem=recv.at[slot],
-                device_id=row_peer(1), device_id_type=MESH).wait_recv()
+                src_ref=buf.at[slot], dst_ref=buf.at[slot], send_sem=send.at[0], recv_sem=sem,
+                device_id=device, device_id_type=MESH)
+
+        def pair_row(q):
+            return lax.rem(r + 2 * q, nrow)
 
         def start():
-            loop(1, ncol, lambda i: to_col(ncol - i).start())
-            for j in range(1, nrow):
-                to_row(0, j).start()
+            def one(i):
+                k = ncol - i
+                for q in range(pairs if i <= ncol - far else 1):
+                    copy(me, recv.at[k, q], (pair_row(q), flipped(c, k, ncol))).start()
+
+            if far == ncol:
+                loop(1, ncol, lambda i: copy(me, recv.at[ncol - i, 0], col_peer(ncol - i)).start())
+            else:
+                for i in range(1, ncol):
+                    one(i)
+            share(r * ncol + c)
+
+        def share(slot):
+            for q in range(1, pairs):
+                copy(slot, rest.at[0], (pair_row(q), c)).start()
+            for q in range(1, pairs):
+                copy(slot, rest.at[0], (lax.rem(partner + 2 * q, nrow), c)).start()
+            copy(slot, rest.at[0], (partner, c)).start()
+
+        def arrival(slot, k, q):
+            copy(slot, recv.at[k, q], (partner, c)).wait_recv()
 
         def relay(first, last):
-            def one(k):
-                arrival(r * ncol + flipped(c, k, ncol))
-                for j in range(1, nrow):
-                    to_row(k, j).start()
-
-            loop(first, last, one)
+            def near(k):
+                slot = r * ncol + flipped(c, k, ncol)
+                arrival(slot, k, 0)
+                share(slot)
+
+            def distant(k):
+                for q in range(pairs):
+                    slot = pair_row(pairs - q) * ncol + flipped(c, k, ncol)
+                    arrival(slot, k, q)
+                    copy(slot, rest.at[0], (partner, c)).start()
+
+            loop(first, min(last, far), near)
+            if last > far:
+                loop(max(first, far), last, distant)
 
         def finish():
-            def one(k):
-                for j in range(1, nrow):
-                    arrival(lax.rem(r + j, nrow) * ncol + flipped(c, k, ncol))
-
-            loop(0, ncol, one)
+            some = buf.at[pl.ds(0, ndev - 1 - singles)]
+            pltpu.make_async_copy(some, some, rest.at[0]).wait()
 
         def drain():
-            def one(k):
-                for j in range(1, nrow):
-                    to_row(k, j).wait_send()
-
-            loop(0, ncol, one)
-            loop(1, ncol, lambda k: to_col(k).wait_send())
+            count = singles + far * (nrow - 1) + (ncol - far) * pairs
+            while count > 0:
+                now = min(count, ndev)
+                some = buf.at[pl.ds(0, now)]
+                pltpu.make_async_copy(some, some, send.at[0]).wait()
+                count -= now
 
         return start, relay, finish, drain
 
@@ -252,12 +271,8 @@
 
         loop(0, ndev // 2, one)
 
-    start1, relay1, finish1, drain1 = spread(gathered, ag1_send, ag1_recv)
+    start1, relay1, finish1, drain1 = spread(gathered, ag1_send, ag1_recv, ag1_rest, ncol)
     start1()
-    for d in range(4):
-        @pl.when(exists[opposite[d]])
-        def _():
-            lend(d).start()
 
     loads[2].wait()
     local = jnp.concatenate([res_ref[...], inc], axis=1)
@@ -279,6 +294,10 @@
     coarse_hi[...] = a_hi
     coarse_lo[...] = a_lo
     finish1()
+    for d in range(4):
+        @pl.when(exists[opposite[d]])
+        def _():
+            lend(d).start()
 
     unpacked(gathered)
     depth = min(total, 2048)
@@ -309,15 +328,8 @@
         peer = flipped(c, k, ncol)
         return pltpu.make_async_remote_copy(
             src_ref=pieces.at[peer], dst_ref=received.at[c],
-            send_sem=rs_send.at[k], recv_sem=rs_recv.at[c],
+            send_sem=rs_send.at[0], recv_sem=rs_recv.at[0],
             device_id=(r, peer), device_id_type=MESH)
-
-    def reduce_arrival(k):
-        peer = flipped(c, k, ncol)
-        pltpu.make_async_remote_copy(
-            src_ref=pieces.at[peer], dst_ref=received.at[peer],
-            send_sem=rs_send.at[k], recv_sem=rs_recv.at[peer],
-            device_id=(r, peer), device_id_type=MESH).wait_recv()
 
     loop(1, ncol, lambda i: reduce(ncol - i).start())
 
@@ -361,7 +373,8 @@
             wide_hi[at] = jnp.where(here, l_hi, jnp.zeros_like(l_hi))
             wide_lo[at] = jnp.where(here, l_lo, jnp.zeros_like(l_lo))
 
-    loop(1, ncol, reduce_arrival)
+    others = received.at[pl.ds(0, ncol - 1)]
+    pltpu.make_async_copy(others, others, rs_recv.at[0]).wait()
     summed = pieces[c]
     if ncol - 1 <= UNROLL:
         for k in range(1, ncol):
@@ -370,7 +383,7 @@
         summed = lax.fori_loop(1, ncol, lambda k, acc: acc + received[flipped(c, k, ncol)], summed)
     solved[me] = summed
 
-    start2, relay2, finish2, drain2 = spread(solved, ag2_send, ag2_recv)
+    start2, relay2, finish2, drain2 = spread(solved, ag2_send, ag2_recv, ag2_rest, ncol * FAR_NUM // FAR_DEN)
     start2()
     relay2(1, ncol)
     finish2()
@@ -389,7 +402,7 @@
 
     drain1()
     drain2()
-    loop(1, ncol, lambda k: reduce(k).wait_send())
+    pltpu.make_async_copy(others, others, rs_send.at[0]).wait()
     for d in range(4):
         @pl.when(exists[d])
         def _():
@@ -444,12 +457,14 @@
             dma((4,)),
             dma((4,)),
             dma((4,)),
-            dma((ncol, nrow)),
-            dma((ndev,)),
-            dma((ncol,)),
-            dma((ncol,)),
-            dma((ncol, nrow)),
-            dma((ndev,)),
+            dma((1,)),
+            dma((ncol, 1)),
+            dma((1,)),
+            dma((1,)),
+            dma((1,)),
+            dma((1,)),
+            dma((ncol, nrow // 2)),
+            dma((1,)),
         ],
         compiler_params=pltpu.CompilerParams(collective_id=0, has_side_effects=True),
     )(

time: 31.2 us -> 29.8 us (0.955)
  Pallas kernels: 30.5 us -> 29 us
    pallas_call x1, Pallas kernels: 30.5 us -> 29 us  [shards(): pl.pallas_call(functools.partial(kernel, nrow, ncol), name='schwarz', out...]
where the time goes in v3:
time: 29.8 us; the launch traced here: 29.6 us
  Pallas kernels  29 us (97%)
  local copies, waits for them, and re-layouts  0.63 us (2%)
    pallas_call x1, Pallas kernels, shards(): pl.pallas_call(functools.partial(kernel, nrow, ncol), name='schwarz', out...  29 us
    unnamed x1, local copies, waits for them, and re-layouts  0.63 us

profile of v3, /device:TPU:0, one launch (start us, length us, event | category | flops | bytes accessed | tf_op | source)
XLA Modules:
  0.0 29.6 jit_solution(16640773471746439877)
XLA Ops:
  0.0 29.0 %schwarz.1 = f32[32,512]{1,0:T(8,128)S(1)} custom-call(bf16[32,512]{1,0:T(8,128)(2,1)} %bitcast.6, s32[1,4]{1,0:T(1,128)} %ib_hbm.1, bf16[512,1024]{1,0:T(8,128)(2,1)} %linv_hbm.1, f32[64,1024]{1,0:T(8,128)} %bitcast.5, s32[1,2048]{1,0:T(1,128)} %bitcast.7, f32[512,256]{1,0:T(8,128)} %coarse_hbm.1), custom_call_target="tpu_custom_call" | custom-call | tf_op jit(solution)/shard_map/schwarz/pallas_call | solution.py:427
  29.0 0.6 %copy.8 = f32[512,32]{0,1:T(8,128)} copy(f32[512,32]{0,1:T(8,128)S(1)} %bitcast.4) | data formatting | bytes 131072

commit v4 on v3

--- a/solution.py
+++ b/solution.py
@@ -11,7 +11,7 @@
 BLK = 128
 LANES = 128
 UNROLL = 16
-FAR_NUM, FAR_DEN = 3, 4
+FAR_NUM, FAR_DEN = 1, 2
 NT = (((1,), (1,)), ((), ()))
 NN = (((1,), (0,)), ((), ()))
 F32 = jnp.float32
@@ -81,13 +81,13 @@
     hot_in,
     hot_out,
     gathered,
-    gathered2,
     pieces,
     received,
     solved,
     lent,
     wide_hi,
     wide_lo,
+    passed,
     load_sem,
     halo_send,
     halo_recv,
@@ -112,6 +112,8 @@
     rows, width = coarse.shape
     total = slots_ref.shape[1]
 
+    near = ncol * FAR_NUM // FAR_DEN
+
     def col_peer(k):
         return (r, flipped(c, k, ncol))
 
@@ -167,6 +169,8 @@
             device_id=target[opposite[d]], device_id_type=MESH)
 
     pl.semaphore_wait(barrier, ncol + nrow - 2)
+    for q in range(1, nrow // 2):
+        pl.semaphore_signal(passed, inc=1, device_id=(lax.rem(r + 2 * q, nrow), c), device_id_type=MESH)
     for d in range(4):
         @pl.when(exists[d])
         def _():
@@ -218,10 +222,10 @@
 
         def share(slot):
             for q in range(1, pairs):
-                copy(slot, rest.at[0], (pair_row(q), c)).start()
+                copy(slot, rest.at[pairs - q], (pair_row(q), c)).start()
             for q in range(1, pairs):
-                copy(slot, rest.at[0], (lax.rem(partner + 2 * q, nrow), c)).start()
-            copy(slot, rest.at[0], (partner, c)).start()
+                copy(slot, rest.at[2 * pairs - q], (lax.rem(partner + 2 * q, nrow), c)).start()
+            copy(slot, rest.at[pairs], (partner, c)).start()
 
         def arrival(slot, k, q):
             copy(slot, recv.at[k, q], (partner, c)).wait_recv()
@@ -236,15 +240,27 @@
                 for q in range(pairs):
                     slot = pair_row(pairs - q) * ncol + flipped(c, k, ncol)
                     arrival(slot, k, q)
-                    copy(slot, rest.at[0], (partner, c)).start()
+                    copy(slot, rest.at[pairs + (pairs - q) % pairs], (partner, c)).start()
 
             loop(first, min(last, far), near)
             if last > far:
                 loop(max(first, far), last, distant)
 
-        def finish():
-            some = buf.at[pl.ds(0, ndev - 1 - singles)]
-            pltpu.make_async_copy(some, some, rest.at[0]).wait()
+        def finish(consume):
+            def wait(index, count):
+                some = buf.at[pl.ds(0, count)]
+                pltpu.make_async_copy(some, some, rest.at[index]).wait()
+
+            total = consume(r, None)
+            wait(pairs, ncol)
+            total = consume(partner, total)
+            for o in range(1, pairs):
+                wait(o, far)
+                total = consume(pair_row(o), total)
+            for o in range(1, pairs):
+                wait(pairs + o, ncol)
+                total = consume(lax.rem(partner + 2 * o, nrow), total)
+            return total
 
         def drain():
             count = singles + far * (nrow - 1) + (ncol - far) * pairs
@@ -256,22 +272,30 @@
 
         return start, relay, finish, drain
 
-    def unpacked(buf):
-        def one(p):
-            a, b = buf[2 * p], buf[2 * p + 1]
-            top = jnp.where(low, a, half_roll(b))
-            bot = jnp.where(low, half_roll(a), b)
-            t_hi, t_lo = split(top)
-            b_hi, b_lo = split(bot)
-            lanes = pl.ds(p * LANES if isinstance(p, int) else pl.multiple_of(p * LANES, LANES), LANES)
-            gathered2[0 * half:1 * half, lanes] = t_hi
-            gathered2[1 * half:2 * half, lanes] = b_hi
-            gathered2[2 * half:3 * half, lanes] = t_lo
-            gathered2[3 * half:4 * half, lanes] = b_lo
-
-        loop(0, ndev // 2, one)
-
-    start1, relay1, finish1, drain1 = spread(gathered, ag1_send, ag1_recv, ag1_rest, ncol)
+    depth = ncol * nev
+
+    def unpacked(buf, row):
+        tops, bots = [], []
+        for p in range(ncol // 2):
+            a, b = buf[row * ncol + 2 * p], buf[row * ncol + 2 * p + 1]
+            tops.append(jnp.where(low, a, half_roll(b)))
+            bots.append(jnp.where(low, half_roll(a), b))
+        value = jnp.concatenate([jnp.concatenate(tops, axis=1), jnp.concatenate(bots, axis=1)], axis=0)
+        return jnp.concatenate(split(value), axis=0)
+
+    def plus(total, part):
+        return part if total is None else total + part
+
+    def take_in(row, total):
+        lanes = pl.ds(pl.multiple_of(row * depth, depth), depth)
+        return plus(total, matmul(unpacked(gathered, row), hot_in[:, lanes], NT))
+
+    def take_out(row, total):
+        at = pl.ds(pl.multiple_of(row * depth, depth), depth)
+        return plus(total, matmul(unpacked(solved, row), hot_out[at], NN))
+
+    start1, relay1, finish1, drain1 = spread(gathered, ag1_send, ag1_recv, ag1_rest, near)
+    pl.semaphore_wait(passed, nrow // 2 - 1)
     start1()
 
     loads[2].wait()
@@ -293,21 +317,12 @@
     a_hi, a_lo = split(coarse[...])
     coarse_hi[...] = a_hi
     coarse_lo[...] = a_lo
-    finish1()
+    column = finish1(take_in)
     for d in range(4):
         @pl.when(exists[opposite[d]])
         def _():
             lend(d).start()
 
-    unpacked(gathered)
-    depth = min(total, 2048)
-    column = matmul(gathered2[:, :depth], hot_in[:, :depth], NT)
-    if total > depth:
-        def more(i, acc):
-            lanes = pl.ds(pl.multiple_of(i * depth, depth), depth)
-            return acc + matmul(gathered2[:, lanes], hot_in[:, lanes], NT)
-
-        column = lax.fori_loop(1, total // depth, more, column)
     column_hi, column_lo = split(column[:rhs] + column[rhs:])
     column2 = jnp.concatenate([column_hi, column_lo], axis=0)
     span = 2 * LANES
@@ -383,18 +398,10 @@
         summed = lax.fori_loop(1, ncol, lambda k, acc: acc + received[flipped(c, k, ncol)], summed)
     solved[me] = summed
 
-    start2, relay2, finish2, drain2 = spread(solved, ag2_send, ag2_recv, ag2_rest, ncol * FAR_NUM // FAR_DEN)
+    start2, relay2, finish2, drain2 = spread(solved, ag2_send, ag2_recv, ag2_rest, near)
     start2()
     relay2(1, ncol)
-    finish2()
-    unpacked(solved)
-    picked = matmul(gathered2[:, :depth], hot_out[:depth], NN)
-    if total > depth:
-        def again(i, acc):
-            at = pl.ds(pl.multiple_of(i * depth, depth), depth)
-            return acc + matmul(gathered2[:, at], hot_out[at], NN)
-
-        picked = lax.fori_loop(1, total // depth, again, picked)
+    picked = finish2(take_out)
     picked = picked.astype(BF16)
 
     inner = matmul(picked, wide_hi[...], NN) + matmul(picked, wide_lo[...], NN)
@@ -445,26 +452,26 @@
             pltpu.VMEM((width, total), BF16),
             pltpu.VMEM((total, 3 * LANES), BF16),
             pltpu.VMEM((ndev,) + packed, F32),
-            pltpu.VMEM((2 * rhs, total), BF16),
             pltpu.VMEM((ncol,) + packed, F32),
             pltpu.VMEM((ncol,) + packed, F32),
             pltpu.VMEM((ndev,) + packed, F32),
             pltpu.VMEM((4, nev, BLK), F32),
             pltpu.VMEM((6 * nev, own), BF16),
             pltpu.VMEM((6 * nev, own), BF16),
+            pltpu.SemaphoreType.REGULAR,
             dma((6,)),
             dma((4,)),
             dma((4,)),
             dma((4,)),
             dma((4,)),
             dma((1,)),
-            dma((ncol, 1)),
-            dma((1,)),
+            dma((ncol, nrow // 2)),
+            dma((nrow,)),
             dma((1,)),
             dma((1,)),
             dma((1,)),
             dma((ncol, nrow // 2)),
-            dma((1,)),
+            dma((nrow,)),
         ],
         compiler_params=pltpu.CompilerParams(collective_id=0, has_side_effects=True),
     )(

time: 29.8 us -> 29.2 us (0.980)
  Pallas kernels: 29 us -> 28.3 us
    pallas_call x1, Pallas kernels: 29 us -> 28.3 us  [shards(): pl.pallas_call(functools.partial(kernel, nrow, ncol), name='schwarz', out...]
where the time goes in v4:
time: 29.2 us; the launch traced here: 28.9 us
  Pallas kernels  28.3 us (97%)
  local copies, waits for them, and re-layouts  0.63 us (2%)
    pallas_call x1, Pallas kernels, shards(): pl.pallas_call(functools.partial(kernel, nrow, ncol), name='schwarz', out...  28.3 us
    unnamed x1, local copies, waits for them, and re-layouts  0.63 us

profile of v4, /device:TPU:0, one launch (start us, length us, event | category | flops | bytes accessed | tf_op | source)
XLA Modules:
  0.0 28.9 jit_solution(14596826944302976237)
XLA Ops:
  0.0 28.3 %schwarz.1 = f32[32,512]{1,0:T(8,128)S(1)} custom-call(bf16[32,512]{1,0:T(8,128)(2,1)} %bitcast.6, s32[1,4]{1,0:T(1,128)} %ib_hbm.1, bf16[512,1024]{1,0:T(8,128)(2,1)} %linv_hbm.1, f32[64,1024]{1,0:T(8,128)} %bitcast.5, s32[1,2048]{1,0:T(1,128)} %bitcast.7, f32[512,256]{1,0:T(8,128)} %coarse_hbm.1), custom_call_target="tpu_custom_call" | custom-call | tf_op jit(solution)/shard_map/schwarz/pallas_call | solution.py:434
  28.3 0.6 %copy.8 = f32[512,32]{0,1:T(8,128)} copy(f32[512,32]{0,1:T(8,128)S(1)} %bitcast.4) | data formatting | bytes 131072

commit v5 on v4

--- a/solution.py
+++ b/solution.py
@@ -327,26 +327,31 @@
     column2 = jnp.concatenate([column_hi, column_lo], axis=0)
     span = 2 * LANES
 
+    def reduce(peer):
+        return pltpu.make_async_remote_copy(
+            src_ref=pieces.at[peer], dst_ref=received.at[c],
+            send_sem=rs_send.at[0], recv_sem=rs_recv.at[0],
+            device_id=(r, peer), device_id_type=MESH)
+
+    group = 2 * (span // LANES)
+
     def product(i):
-        at = pl.ds(i * span if isinstance(i, int) else pl.multiple_of(i * span, span), span)
+        block = lax.rem(c // group + 1 + i, rows // span)
+        at = pl.ds(pl.multiple_of(block * span, span), span)
         part = matmul(column2, coarse_hi[at], NT) + matmul(column2, coarse_lo[at], NT)
         part = part[:rhs] + part[rhs:]
         for q in range(span // LANES):
             top = part[:half, q * LANES:(q + 1) * LANES]
             bot = part[half:, q * LANES:(q + 1) * LANES]
-            pieces[(span // LANES * i + q) * 2] = jnp.where(low, top, half_roll(bot))
-            pieces[(span // LANES * i + q) * 2 + 1] = jnp.where(low, half_roll(top), bot)
+            pieces[block * group + 2 * q] = jnp.where(low, top, half_roll(bot))
+            pieces[block * group + 2 * q + 1] = jnp.where(low, half_roll(top), bot)
+
+        for q in range(group):
+            @pl.when(block * group + q != c)
+            def _():
+                reduce(block * group + q).start()
 
     loop(0, rows // span, product)
-
-    def reduce(k):
-        peer = flipped(c, k, ncol)
-        return pltpu.make_async_remote_copy(
-            src_ref=pieces.at[peer], dst_ref=received.at[c],
-            send_sem=rs_send.at[0], recv_sem=rs_recv.at[0],
-            device_id=(r, peer), device_id_type=MESH)
-
-    loop(1, ncol, lambda i: reduce(ncol - i).start())
 
     low8 = lane_low((8, LANES))
 

time: 29.2 us -> 29.1 us (level)
  no operation moved by 1% of the time
where the time goes in v5:
time: 29.1 us; the launch traced here: 28.8 us
  Pallas kernels  28.1 us (97%)
  local copies, waits for them, and re-layouts  0.63 us (2%)
    pallas_call x1, Pallas kernels, shards(): pl.pallas_call(functools.partial(kernel, nrow, ncol), name='schwarz', out...  28.1 us
    unnamed x1, local copies, waits for them, and re-layouts  0.63 us

profile of v5, /device:TPU:0, one launch (start us, length us, event | category | flops | bytes accessed | tf_op | source)
XLA Modules:
  0.0 28.8 jit_solution(4928702994666101671)
XLA Ops:
  0.0 28.1 %schwarz.1 = f32[32,512]{1,0:T(8,128)S(1)} custom-call(bf16[32,512]{1,0:T(8,128)(2,1)} %bitcast.6, s32[1,4]{1,0:T(1,128)} %ib_hbm.1, bf16[512,1024]{1,0:T(8,128)(2,1)} %linv_hbm.1, f32[64,1024]{1,0:T(8,128)} %bitcast.5, s32[1,2048]{1,0:T(1,128)} %bitcast.7, f32[512,256]{1,0:T(8,128)} %coarse_hbm.1), custom_call_target="tpu_custom_call" | custom-call | tf_op jit(solution)/shard_map/schwarz/pallas_call | solution.py:439
  28.1 0.6 %copy.8 = f32[512,32]{0,1:T(8,128)} copy(f32[512,32]{0,1:T(8,128)S(1)} %bitcast.4) | data formatting | bytes 131072
